TPU v7x, 32 devices: a whole 2x2x4 slice. The times are simulated.
32 devices in a mesh: rep: 2 (over x), blk: 16 (over z, y, core).
Axes of the slice: x: 2, y: 2, z: 4, core: 2. Of those that a mesh axis runs over, the one named last changes fastest.
Arguments:
- positions: float32 [3, 8192], P(None, ('rep', 'blk')), parts along dimension 1, may hold values from 0 to 64
- forces: float32 [6, 3, 8192], P(None, None, ('rep', 'blk')), parts along dimension 2, may hold values from -6 to 6
- random_kicks: float32 [6, 3, 8192], P(None, None, ('rep', 'blk')), parts along dimension 2, may hold values from -4 to 4
- history_velocity: float32 [128, 3, 8192], P(None, None, ('rep', 'blk')), parts along dimension 2, may hold values from -6 to 6
- history_offset: float32 [128, 3, 8192], P(None, None, ('rep', 'blk')), parts along dimension 2, may hold values from -8 to 8
- lag_index: int32 [4096], P(('rep', 'blk')), parts along dimension 0, may hold values from 0 to 127
Outputs:
- final_positions: float32 [3, 8192], P(None, ('rep', 'blk')), parts along dimension 1
- velocity: float32 [3, 8192], P(None, ('rep', 'blk')), parts along dimension 1
- statistics: float32 [2, 4096], P(None, ('rep', 'blk')), parts along dimension 1
There are 2 independent parts, one for each index of `rep`. A program takes and returns all parts, laid end to end along the dimension named above; each array names one. Nothing has to cross between parts.
All inputs are finite; a program needn't handle non-finite values.
Results may differ from a plain program's by a relative error of at most 0.0003.
Values sent between devices are 32-bit elements; how exact they have to be, the bound alone decides.
A program may use at most 64 MiB of HBM per device.

v0:
```python
import math
import jax
import jax.numpy as jnp
from jax import lax
from jax.sharding import PartitionSpec as P

STEPS = 6
time_step = 0.05


def pair_coefs(targets, sources):
    separation = targets[:, None, :] - sources[:, :, None]
    dist_sq = jnp.sum(separation * separation, axis=0)
    dist_safe = jnp.where(dist_sq > 0.0, dist_sq, 1.0)
    inv_dist = lax.rsqrt(dist_safe)
    distance = dist_sq * inv_dist
    inv_sq = 1.0 / dist_safe
    far_mask = distance >= 2.0
    coef_iso = jnp.where(
        far_mask, 0.75 * inv_dist * (1.0 + 2.0 / 3.0 * inv_sq), 1.0 - 9.0 / 32.0 * distance
    )
    coef_dir = jnp.where(
        far_mask, 0.75 * inv_dist * (1.0 - 2.0 * inv_sq) * inv_sq, 3.0 / 32.0 * inv_dist
    )
    return (separation, coef_iso, coef_dir)


def pair_velocity(targets, sources, loads):
    separation, coef_iso, coef_dir = pair_coefs(targets, sources)
    projection = jnp.sum(separation * loads[:, :, None], axis=0)
    return jnp.sum(
        coef_iso[None] * loads[:, :, None] + (coef_dir * projection)[None] * separation, axis=1
    )


def blockwise(targets, sources, loads):
    source_count = sources.shape[1]
    row_count = math.gcd(source_count, 512)
    block_count = source_count // row_count
    source_blocks = sources.reshape(3, block_count, row_count).transpose(1, 0, 2)
    load_blocks = loads.reshape(3, block_count, row_count).transpose(1, 0, 2)

    def accumulate(running, source_block):
        return (running + pair_velocity(targets, source_block[0], source_block[1]), None)

    running, unused = lax.scan(
        accumulate, jnp.zeros(targets.shape, jnp.float32), (source_blocks, load_blocks)
    )
    return running


def local(positions, forces, random_kicks, history_velocity, history_offset, lag_index):
    places = positions
    velocity = jnp.zeros_like(positions)
    all_forces = lax.all_gather(forces, "blk", axis=2, tiled=True)
    for step_index in range(STEPS):
        targets = places
        step_forces = all_forces[step_index]
        velocity = blockwise(
            targets, lax.all_gather(targets, "blk", axis=1, tiled=True), step_forces
        )
        places = places + time_step * velocity + random_kicks[step_index]
    velocity_dot = jnp.sum(velocity[None] * history_velocity, axis=(1, 2))
    moved = places[None] - positions[None] - history_offset
    square_disp = jnp.sum(moved * moved, axis=(1, 2))
    frames = history_velocity.shape[0]
    sphere_total = jnp.float32(positions.shape[1] * lax.axis_size("blk"))
    every_lag = lax.all_gather(lag_index, "blk", axis=0, tiled=True)
    onehot = (every_lag[:, None] == jnp.arange(frames, dtype=jnp.int32)[None, :]).astype(
        jnp.float32
    )
    frame_table = jnp.stack([velocity_dot, square_disp], axis=0)
    local_terms = jnp.dot(
        frame_table, onehot.T, precision=lax.Precision.HIGHEST, preferred_element_type=jnp.float32
    )
    statistics = (
        lax.psum_scatter(local_terms, "blk", scatter_dimension=1, tiled=True) / sphere_total
    )
    return (places, velocity, statistics)


def solution(mesh):
    return jax.shard_map(
        local,
        mesh=mesh,
        in_specs=(
            P(None, ("rep", "blk")),
            P(None, None, ("rep", "blk")),
            P(None, None, ("rep", "blk")),
            P(None, None, ("rep", "blk")),
            P(None, None, ("rep", "blk")),
            P(("rep", "blk")),
        ),
        out_specs=(P(None, ("rep", "blk")), P(None, ("rep", "blk")), P(None, ("rep", "blk"))),
        check_vma=False,
    )
```

profile of v0, /device:TPU:0, one launch (start us, length us, event | category | flops | bytes accessed | tf_op | source)
XLA Modules:
  0.0 293.1 jit_solution(7134342505187755510)
XLA Ops:
  7.3 24.4 %all_gather.25 = f32[6,3,4096]{2,1,0:T(4,128)S(1)} all-gather(f32[6,3,256]{2,1,0:T(4,128)} %param.19), channel_id=1, replica_groups=mesh['rep'=2,'blk'=16] {'blk'}, dimensions={2}, use_global_device_ids=true | all-gather | bytes 313344 | tf_op jit(solution)/shard_map/all_gather | solution.py:55
  31.8 17.6 %all_gather.24 = f32[3,4096]{1,0:T(4,128)S(1)} all-gather(f32[3,256]{1,0:T(4,128)S(1)} %copy-done), channel_id=1, replica_groups=mesh['rep'=2,'blk'=16] {'blk'}, dimensions={1}, use_global_device_ids=true | all-gather | bytes 52224 | tf_op jit(solution)/shard_map/all_gather | solution.py:60
  49.4 11.2 %while.66 = (s32[]{:T(128)}, f32[3,256]{1,0:T(4,128)S(1)}, f32[3,256]{1,0:T(4,128)S(1)}, f32[8,3,512]{2,1,0:T(4,128)S(1)}, f32[8,3,512]{2,1,0:T(4,128)S(1)}, /*index=5*/s32[]{:T(128)}, s32[]{:T(128)}) while((s32[]{:T(128)}, f32[3,256]{1,0:T(4,128)S(1)}, f32[3,256]{1,0:T(4,128)S(1)}, f32[8,3,512]{2,1,0:T(4,128)S(1)}, ...), condition=%wide.region_4.5_spmd.clone, body=%wide.region_0.4_spmd.clone.sunk | while | flops 6161155 | bytes 4261979 | solution.py:46
  50.3 0.5 fusion.68
  51.7 0.5 fusion.68
  53.1 0.5 fusion.68
  54.5 0.5 fusion.68
  55.9 0.5 fusion.68
  60.6 18.9 %all_gather.26 = f32[3,4096]{1,0:T(4,128)S(1)} all-gather(f32[3,256]{1,0:T(4,128)S(1)} %bitcast_add_fusion.5), channel_id=1, replica_groups=mesh['rep'=2,'blk'=16] {'blk'}, dimensions={1}, use_global_device_ids=true | all-gather | bytes 52224 | tf_op jit(solution)/shard_map/all_gather | solution.py:60
  79.5 11.2 %while.67 = (s32[]{:T(128)}, f32[3,256]{1,0:T(4,128)S(1)}, f32[3,256]{1,0:T(4,128)S(1)}, f32[8,3,512]{2,1,0:T(4,128)S(1)}, f32[8,3,512]{2,1,0:T(4,128)S(1)}, /*index=5*/s32[]{:T(128)}, s32[]{:T(128)}) while((s32[]{:T(128)}, f32[3,256]{1,0:T(4,128)S(1)}, f32[3,256]{1,0:T(4,128)S(1)}, f32[8,3,512]{2,1,0:T(4,128)S(1)}, ...), condition=%wide.region_9.10_spmd.clone, body=%wide.region_5.9_spmd.clone.sunk | while | flops 6161155 | bytes 4261979 | solution.py:46
  90.7 17.6 %all_gather.27 = f32[3,4096]{1,0:T(4,128)S(1)} all-gather(f32[3,256]{1,0:T(4,128)S(1)} %bitcast_add_fusion.4), channel_id=1, replica_groups=mesh['rep'=2,'blk'=16] {'blk'}, dimensions={1}, use_global_device_ids=true | all-gather | bytes 52224 | tf_op jit(solution)/shard_map/all_gather | solution.py:60
  108.3 11.2 %while.68 = (s32[]{:T(128)}, f32[3,256]{1,0:T(4,128)S(1)}, f32[3,256]{1,0:T(4,128)S(1)}, f32[8,3,512]{2,1,0:T(4,128)S(1)}, f32[8,3,512]{2,1,0:T(4,128)S(1)}, /*index=5*/s32[]{:T(128)}, s32[]{:T(128)}) while((s32[]{:T(128)}, f32[3,256]{1,0:T(4,128)S(1)}, f32[3,256]{1,0:T(4,128)S(1)}, f32[8,3,512]{2,1,0:T(4,128)S(1)}, ...), condition=%wide.region_14.15_spmd.clone, body=%wide.region_10.14_spmd.clone.sunk | while | flops 6161155 | bytes 4261979 | solution.py:46
  119.5 18.9 %all_gather.28 = f32[3,4096]{1,0:T(4,128)S(1)} all-gather(f32[3,256]{1,0:T(4,128)S(1)} %bitcast_add_fusion.3), channel_id=1, replica_groups=mesh['rep'=2,'blk'=16] {'blk'}, dimensions={1}, use_global_device_ids=true | all-gather | bytes 52224 | tf_op jit(solution)/shard_map/all_gather | solution.py:60
  138.5 11.2 %while.69 = (s32[]{:T(128)}, f32[3,256]{1,0:T(4,128)S(1)}, f32[3,256]{1,0:T(4,128)S(1)}, f32[8,3,512]{2,1,0:T(4,128)S(1)}, f32[8,3,512]{2,1,0:T(4,128)S(1)}, /*index=5*/s32[]{:T(128)}, s32[]{:T(128)}) while((s32[]{:T(128)}, f32[3,256]{1,0:T(4,128)S(1)}, f32[3,256]{1,0:T(4,128)S(1)}, f32[8,3,512]{2,1,0:T(4,128)S(1)}, ...), condition=%wide.region_19.20_spmd.clone, body=%wide.region_15.19_spmd.clone.sunk | while | flops 6161155 | bytes 4261979 | solution.py:46
  149.6 17.6 %all_gather.29 = f32[3,4096]{1,0:T(4,128)S(1)} all-gather(f32[3,256]{1,0:T(4,128)S(1)} %bitcast_add_fusion.2), channel_id=1, replica_groups=mesh['rep'=2,'blk'=16] {'blk'}, dimensions={1}, use_global_device_ids=true | all-gather | bytes 52224 | tf_op jit(solution)/shard_map/all_gather | solution.py:60
  167.3 11.1 %while.70 = (s32[]{:T(128)}, f32[3,256]{1,0:T(4,128)S(1)}, f32[3,256]{1,0:T(4,128)S(1)}, f32[8,3,512]{2,1,0:T(4,128)S(1)}, f32[8,3,512]{2,1,0:T(4,128)S(1)}, /*index=5*/s32[]{:T(128)}, s32[]{:T(128)}) while((s32[]{:T(128)}, f32[3,256]{1,0:T(4,128)S(1)}, f32[3,256]{1,0:T(4,128)S(1)}, f32[8,3,512]{2,1,0:T(4,128)S(1)}, ...), condition=%wide.region_24.25_spmd.clone, body=%wide.region_20.24_spmd.clone.sunk | while | flops 6161155 | bytes 4261979 | solution.py:46
  178.4 18.9 %all_gather.30 = f32[3,4096]{1,0:T(4,128)S(1)} all-gather(f32[3,256]{1,0:T(4,128)S(1)} %bitcast_add_fusion.1), channel_id=1, replica_groups=mesh['rep'=2,'blk'=16] {'blk'}, dimensions={1}, use_global_device_ids=true | all-gather | bytes 52224 | tf_op jit(solution)/shard_map/all_gather | solution.py:60
  197.4 11.2 %while.71 = (s32[]{:T(128)}, f32[3,256]{1,0:T(4,128)S(1)}, f32[3,256]{1,0:T(4,128)S(1)}, f32[8,3,512]{2,1,0:T(4,128)S(1)}, f32[8,3,512]{2,1,0:T(4,128)S(1)}, /*index=5*/s32[]{:T(128)}, s32[]{:T(128)}) while((s32[]{:T(128)}, f32[3,256]{1,0:T(4,128)S(1)}, f32[3,256]{1,0:T(4,128)S(1)}, f32[8,3,512]{2,1,0:T(4,128)S(1)}, ...), condition=%wide.region_29.30_spmd.clone, body=%wide.region_25.29_spmd.clone.sunk | while | flops 6161155 | bytes 4261979 | solution.py:46
  208.5 0.6 fusion.53
  209.3 17.5 %all-gather = s32[16,1,128]{2,1,0:T(1,128)S(1)} all-gather(s32[1,1,128]{2,1,0:T(1,128)S(1)} %bitcast.108), channel_id=1, replica_groups=mesh['rep'=2,'blk'=16] {'blk'}, dimensions={0}, use_global_device_ids=true | all-gather | bytes 8704 | tf_op jit(solution)/shard_map/all_gather | solution.py:68
  226.8 1.7 convolution_bitcast_fusion
  228.6 56.2 %reduce-scatter.4.cloned.1.call-done = f32[128,2]{1,0:T(8,128)} async-done(((f32[2048,2]{1,0:T(8,128)}), f32[128,2]{1,0:T(8,128)}) %reduce-scatter.4.cloned.1.call-update) | async-done | bytes 1040
  284.8 0.9 copy.25
  285.7 0.6 broadcast_multiply_fusion
  (263 shorter events, 62.7 us)
Async XLA Ops:
  7.2 24.6 %copy-start = (f32[3,256]{1,0:T(4,128)S(1)}, f32[3,256]{1,0:T(4,128)}, u32[]{:S(2)}) copy-start(f32[3,256]{1,0:T(4,128)} %param.18) | copy-start | bytes 9220
  7.2 277.6 %reduce-scatter.4.cloned.1.call-start = ((), (), s32[]{:S(2)}) async-start(), calls=%async_computation.1 | async-start | bytes 1114112
  49.4 11.2 %copy-start.4 = (f32[6,3,256]{2,1,0:T(4,128)S(1)}, f32[6,3,256]{2,1,0:T(4,128)}, u32[]{:S(2)}) copy-start(f32[6,3,256]{2,1,0:T(4,128)} %param.20) | copy-start | bytes 55300
  197.3 11.8 %copy-start.1 = (f32[128,3,256]{2,0,1:T(8,128)S(1)}, f32[128,3,256]{2,0,1:T(8,128)}, u32[]{:S(2)}) copy-start(f32[128,3,256]{2,0,1:T(8,128)} %param.21) | copy-start | bytes 1179652
  197.3 11.9 %copy-start.5 = (s32[128]{0:T(128)S(1)}, s32[128]{0:T(128)}, u32[]{:S(2)}) copy-start(s32[128]{0:T(128)} %param.23) | copy-start | bytes 1540
  197.3 29.4 %copy-start.2 = (f32[128,3,256]{2,0,1:T(8,128)S(1)}, f32[128,3,256]{2,0,1:T(8,128)}, u32[]{:S(2)}) copy-start(f32[128,3,256]{2,0,1:T(8,128)} %param.22) | copy-start | bytes 1179652
  208.5 20.1 %copy-start.3 = (f32[3,256]{1,0:T(4,128)}, f32[3,256]{1,0:T(4,128)S(1)}, u32[]{:S(2)}) copy-start(f32[3,256]{1,0:T(4,128)S(1)} %get-tuple-element.163) | copy-start | bytes 9220
Sparse Core Ops, SparseCore 0:
  228.7 56.0 reduce-scatter.3
where the time goes:
time: 293 us
  blocking collectives  152 us (52%)
  other arithmetic  65.7 us (22%)
  waiting for transfers between devices  56.2 us (19%)
  between operations  14.2 us (5%)
    all_gather x6, blocking collectives, local(): lax.all_gather(targets, 'blk', axis=1, tiled=True)  110 us
    unnamed x2, waiting for transfers between devices  56.2 us
    all_gather x1, blocking collectives, local(): all_forces = lax.all_gather(forces, 'blk', axis=2, tiled=True)  24.4 us
    reduce_sum x48, other arithmetic, pair_velocity(): jnp.sum(coef_iso[None] * loads[:, :, None] + (coef_dir * projection)[None...  23.4 us
    reduce_sum x48, other arithmetic, pair_coefs(): dist_sq = jnp.sum(separation * separation, axis=0)  22.6 us
    select_n x48, other arithmetic, pair_coefs(): jnp.where(far_mask, 0.75 * inv_dist * (1.0 + 2.0 / 3.0 * inv_sq), 1.0 - 9...  17.6 us
    all_gather x1, blocking collectives, local(): every_lag = lax.all_gather(lag_index, 'blk', axis=0, tiled=True)  17.5 us
  transfers between devices with their start and end apart: 1, of which 1 were waited for; matrix products, arithmetic and copies ran while one was open for 0% of the time, Pallas kernels for 0%

commit v1 on v0

--- a/solution.py
+++ b/solution.py
@@ -6,6 +6,17 @@
 
 STEPS = 6
 time_step = 0.05
+
+
+def gather_by_hops(array, axis, d):
+    size = lax.axis_size(axis)
+    right = [(i, (i + 1) % size) for i in range(size)]
+    parts = [array]
+    for hop in range(1, size):
+        parts = [lax.ppermute(parts[0], axis, right), *parts]
+    full = jnp.concatenate(parts, axis=d)
+    shift = (lax.axis_index(axis) + 1) * parts[-1].shape[d]
+    return jnp.roll(full, shift, axis=d)
 
 
 def pair_coefs(targets, sources):
@@ -52,7 +63,7 @@
 def local(positions, forces, random_kicks, history_velocity, history_offset, lag_index):
     places = positions
     velocity = jnp.zeros_like(positions)
-    all_forces = lax.all_gather(forces, "blk", axis=2, tiled=True)
+    all_forces = gather_by_hops(forces, "blk", 2)
     for step_index in range(STEPS):
         targets = places
         step_forces = all_forces[step_index]

time: 293 us -> 350 us (1.19)
  waiting for transfers between devices: 56.2 us -> 134 us
  blocking collectives: 152 us -> 128 us
    ppermute x0 -> x15, waiting for transfers between devices: none -> 78.1 us  [gather_by_hops(): parts = [lax.ppermute(parts[0], axis, right), *parts]]
    all_gather x1 -> x0, blocking collectives: 24.4 us -> none  [local(): all_forces = lax.all_gather(forces, 'blk', axis=2, tiled=True)]
  transfers between devices with their start and end apart: 1 -> 16, of which waited for: 1 -> 14; matrix products, arithmetic and copies ran while one was open for 0% -> 0% of each run, Pallas kernels for 0% -> 0%
where the time goes in v1:
time: 350 us
  waiting for transfers between devices  134 us (38%)
  blocking collectives  128 us (37%)
  other arithmetic  65.7 us (19%)
  between operations  14.4 us (4%)
    all_gather x6, blocking collectives, local(): lax.all_gather(targets, 'blk', axis=1, tiled=True)  110 us
    ppermute x15, waiting for transfers between devices, gather_by_hops(): parts = [lax.ppermute(parts[0], axis, right), *parts]  78.1 us
    unnamed x2, waiting for transfers between devices  56.3 us
    reduce_sum x48, other arithmetic, pair_velocity(): jnp.sum(coef_iso[None] * loads[:, :, None] + (coef_dir * projection)[None...  23.4 us
    reduce_sum x48, other arithmetic, pair_coefs(): dist_sq = jnp.sum(separation * separation, axis=0)  22.6 us
    all_gather x1, blocking collectives, local(): every_lag = lax.all_gather(lag_index, 'blk', axis=0, tiled=True)  18.1 us
    select_n x48, other arithmetic, pair_coefs(): jnp.where(far_mask, 0.75 * inv_dist * (1.0 + 2.0 / 3.0 * inv_sq), 1.0 - 9...  17.6 us
  transfers between devices with their start and end apart: 16, of which 14 were waited for; matrix products, arithmetic and copies ran while one was open for 0% of the time, Pallas kernels for 0%

profile of v1, /device:TPU:0, one launch (start us, length us, event | category | flops | bytes accessed | tf_op | source)
XLA Modules:
  0.0 349.9 jit_solution(2095513304598115798)
XLA Ops:
  7.8 6.7 %collective-permute-done = f32[6,3,256]{2,1,0:T(4,128)S(1)} collective-permute-done((f32[6,3,256]{2,1,0:T(4,128)}, f32[6,3,256]{2,1,0:T(4,128)S(1)}, u32[]{:S(2)}, u32[]{:S(2)}) %collective-permute-start) | collective-permute-done | bytes 18464 | tf_op jit(solution)/shard_map/ppermute | solution.py:16
  14.5 5.9 %collective-permute-done.1 = f32[6,3,256]{2,1,0:T(4,128)S(1)} collective-permute-done((f32[6,3,256]{2,1,0:T(4,128)S(1)}, f32[6,3,256]{2,1,0:T(4,128)S(1)}, u32[]{:S(2)}, u32[]{:S(2)}) %collective-permute-start.1) | collective-permute-done | bytes 18464 | tf_op jit(solution)/shard_map/ppermute | solution.py:16
  20.4 5.9 %collective-permute-done.2 = f32[6,3,256]{2,1,0:T(4,128)S(1)} collective-permute-done((f32[6,3,256]{2,1,0:T(4,128)S(1)}, f32[6,3,256]{2,1,0:T(4,128)S(1)}, u32[]{:S(2)}, u32[]{:S(2)}) %collective-permute-start.2) | collective-permute-done | bytes 18464 | tf_op jit(solution)/shard_map/ppermute | solution.py:16
  26.4 5.9 %collective-permute-done.3 = f32[6,3,256]{2,1,0:T(4,128)S(1)} collective-permute-done((f32[6,3,256]{2,1,0:T(4,128)S(1)}, f32[6,3,256]{2,1,0:T(4,128)S(1)}, u32[]{:S(2)}, u32[]{:S(2)}) %collective-permute-start.3) | collective-permute-done | bytes 18464 | tf_op jit(solution)/shard_map/ppermute | solution.py:16
  32.3 5.9 %collective-permute-done.4 = f32[6,3,256]{2,1,0:T(4,128)S(1)} collective-permute-done((f32[6,3,256]{2,1,0:T(4,128)S(1)}, f32[6,3,256]{2,1,0:T(4,128)S(1)}, u32[]{:S(2)}, u32[]{:S(2)}) %collective-permute-start.4) | collective-permute-done | bytes 18464 | tf_op jit(solution)/shard_map/ppermute | solution.py:16
  38.3 5.9 %collective-permute-done.5 = f32[6,3,256]{2,1,0:T(4,128)S(1)} collective-permute-done((f32[6,3,256]{2,1,0:T(4,128)S(1)}, f32[6,3,256]{2,1,0:T(4,128)S(1)}, u32[]{:S(2)}, u32[]{:S(2)}) %collective-permute-start.5) | collective-permute-done | bytes 18464 | tf_op jit(solution)/shard_map/ppermute | solution.py:16
  56.1 5.9 %collective-permute-done.8 = f32[6,3,256]{2,1,0:T(4,128)S(1)} collective-permute-done((f32[6,3,256]{2,1,0:T(4,128)S(1)}, f32[6,3,256]{2,1,0:T(4,128)S(1)}, u32[]{:S(2)}, u32[]{:S(2)}) %collective-permute-start.8) | collective-permute-done | bytes 18464 | tf_op jit(solution)/shard_map/ppermute | solution.py:16
  62.1 5.9 %collective-permute-done.9 = f32[6,3,256]{2,1,0:T(4,128)S(1)} collective-permute-done((f32[6,3,256]{2,1,0:T(4,128)S(1)}, f32[6,3,256]{2,1,0:T(4,128)S(1)}, u32[]{:S(2)}, u32[]{:S(2)}) %collective-permute-start.9) | collective-permute-done | bytes 18464 | tf_op jit(solution)/shard_map/ppermute | solution.py:16
  74.0 5.9 %collective-permute-done.11 = f32[6,3,256]{2,1,0:T(4,128)S(1)} collective-permute-done((f32[6,3,256]{2,1,0:T(4,128)S(1)}, f32[6,3,256]{2,1,0:T(4,128)S(1)}, u32[]{:S(2)}, u32[]{:S(2)}) %collective-permute-start.11) | collective-permute-done | bytes 18464 | tf_op jit(solution)/shard_map/ppermute | solution.py:16
  79.9 5.9 %collective-permute-done.12 = f32[6,3,256]{2,1,0:T(4,128)S(1)} collective-permute-done((f32[6,3,256]{2,1,0:T(4,128)S(1)}, f32[6,3,256]{2,1,0:T(4,128)S(1)}, u32[]{:S(2)}, u32[]{:S(2)}) %collective-permute-start.12) | collective-permute-done | bytes 18464 | tf_op jit(solution)/shard_map/ppermute | solution.py:16
  85.9 18.1 %all-gather = s32[16,1,128]{2,1,0:T(1,128)S(1)} all-gather(s32[1,1,128]{2,1,0:T(1,128)} %bitcast.108), channel_id=1, replica_groups=mesh['rep'=2,'blk'=16] {'blk'}, dimensions={0}, use_global_device_ids=true | all-gather | bytes 8704 | tf_op jit(solution)/shard_map/all_gather | solution.py:79
  104.2 18.9 %all_gather.21 = f32[3,4096]{1,0:T(4,128)S(1)} all-gather(f32[3,256]{1,0:T(4,128)} %param.18), channel_id=1, replica_groups=mesh['rep'=2,'blk'=16] {'blk'}, dimensions={1}, use_global_device_ids=true | all-gather | bytes 52224 | tf_op jit(solution)/shard_map/all_gather | solution.py:71
  124.5 11.2 %while.66 = (s32[]{:T(128)}, f32[3,256]{1,0:T(4,128)S(1)}, f32[3,256]{1,0:T(4,128)S(1)}, f32[8,3,512]{2,1,0:T(4,128)S(1)}, f32[8,3,512]{2,1,0:T(4,128)S(1)}, /*index=5*/s32[]{:T(128)}, s32[]{:T(128)}) while((s32[]{:T(128)}, f32[3,256]{1,0:T(4,128)S(1)}, f32[3,256]{1,0:T(4,128)S(1)}, f32[8,3,512]{2,1,0:T(4,128)S(1)}, ...), condition=%wide.region_4.5_spmd.clone, body=%wide.region_0.4_spmd.clone.sunk | while | flops 6161155 | bytes 4261979 | solution.py:57
  135.7 17.9 %all_gather.22 = f32[3,4096]{1,0:T(4,128)S(1)} all-gather(f32[3,256]{1,0:T(4,128)S(1)} %bitcast_add_fusion.5), channel_id=1, replica_groups=mesh['rep'=2,'blk'=16] {'blk'}, dimensions={1}, use_global_device_ids=true | all-gather | bytes 52224 | tf_op jit(solution)/shard_map/all_gather | solution.py:71
  153.6 11.2 %while.67 = (s32[]{:T(128)}, f32[3,256]{1,0:T(4,128)S(1)}, f32[3,256]{1,0:T(4,128)S(1)}, f32[8,3,512]{2,1,0:T(4,128)S(1)}, f32[8,3,512]{2,1,0:T(4,128)S(1)}, /*index=5*/s32[]{:T(128)}, s32[]{:T(128)}) while((s32[]{:T(128)}, f32[3,256]{1,0:T(4,128)S(1)}, f32[3,256]{1,0:T(4,128)S(1)}, f32[8,3,512]{2,1,0:T(4,128)S(1)}, ...), condition=%wide.region_9.10_spmd.clone, body=%wide.region_5.9_spmd.clone.sunk | while | flops 6161155 | bytes 4261979 | solution.py:57
  164.8 18.7 %all_gather.23 = f32[3,4096]{1,0:T(4,128)S(1)} all-gather(f32[3,256]{1,0:T(4,128)S(1)} %bitcast_add_fusion.4), channel_id=1, replica_groups=mesh['rep'=2,'blk'=16] {'blk'}, dimensions={1}, use_global_device_ids=true | all-gather | bytes 52224 | tf_op jit(solution)/shard_map/all_gather | solution.py:71
  183.4 11.2 %while.68 = (s32[]{:T(128)}, f32[3,256]{1,0:T(4,128)S(1)}, f32[3,256]{1,0:T(4,128)S(1)}, f32[8,3,512]{2,1,0:T(4,128)S(1)}, f32[8,3,512]{2,1,0:T(4,128)S(1)}, /*index=5*/s32[]{:T(128)}, s32[]{:T(128)}) while((s32[]{:T(128)}, f32[3,256]{1,0:T(4,128)S(1)}, f32[3,256]{1,0:T(4,128)S(1)}, f32[8,3,512]{2,1,0:T(4,128)S(1)}, ...), condition=%wide.region_14.15_spmd.clone, body=%wide.region_10.14_spmd.clone.sunk | while | flops 6161155 | bytes 4261979 | solution.py:57
  194.6 17.9 %all_gather.24 = f32[3,4096]{1,0:T(4,128)S(1)} all-gather(f32[3,256]{1,0:T(4,128)S(1)} %bitcast_add_fusion.3), channel_id=1, replica_groups=mesh['rep'=2,'blk'=16] {'blk'}, dimensions={1}, use_global_device_ids=true | all-gather | bytes 52224 | tf_op jit(solution)/shard_map/all_gather | solution.py:71
  212.5 11.2 %while.69 = (s32[]{:T(128)}, f32[3,256]{1,0:T(4,128)S(1)}, f32[3,256]{1,0:T(4,128)S(1)}, f32[8,3,512]{2,1,0:T(4,128)S(1)}, f32[8,3,512]{2,1,0:T(4,128)S(1)}, /*index=5*/s32[]{:T(128)}, s32[]{:T(128)}) while((s32[]{:T(128)}, f32[3,256]{1,0:T(4,128)S(1)}, f32[3,256]{1,0:T(4,128)S(1)}, f32[8,3,512]{2,1,0:T(4,128)S(1)}, ...), condition=%wide.region_19.20_spmd.clone, body=%wide.region_15.19_spmd.clone.sunk | while | flops 6161155 | bytes 4261979 | solution.py:57
  223.7 18.7 %all_gather.25 = f32[3,4096]{1,0:T(4,128)S(1)} all-gather(f32[3,256]{1,0:T(4,128)S(1)} %bitcast_add_fusion.2), channel_id=1, replica_groups=mesh['rep'=2,'blk'=16] {'blk'}, dimensions={1}, use_global_device_ids=true | all-gather | bytes 52224 | tf_op jit(solution)/shard_map/all_gather | solution.py:71
  242.3 11.1 %while.70 = (s32[]{:T(128)}, f32[3,256]{1,0:T(4,128)S(1)}, f32[3,256]{1,0:T(4,128)S(1)}, f32[8,3,512]{2,1,0:T(4,128)S(1)}, f32[8,3,512]{2,1,0:T(4,128)S(1)}, /*index=5*/s32[]{:T(128)}, s32[]{:T(128)}) while((s32[]{:T(128)}, f32[3,256]{1,0:T(4,128)S(1)}, f32[3,256]{1,0:T(4,128)S(1)}, f32[8,3,512]{2,1,0:T(4,128)S(1)}, ...), condition=%wide.region_24.25_spmd.clone, body=%wide.region_20.24_spmd.clone.sunk | while | flops 6161155 | bytes 4261979 | solution.py:57
  253.5 18.1 %all_gather.26 = f32[3,4096]{1,0:T(4,128)S(1)} all-gather(f32[3,256]{1,0:T(4,128)S(1)} %bitcast_add_fusion.1), channel_id=1, replica_groups=mesh['rep'=2,'blk'=16] {'blk'}, dimensions={1}, use_global_device_ids=true | all-gather | bytes 52224 | tf_op jit(solution)/shard_map/all_gather | solution.py:71
  271.6 11.2 %while.71 = (s32[]{:T(128)}, f32[3,256]{1,0:T(4,128)S(1)}, f32[3,256]{1,0:T(4,128)S(1)}, f32[8,3,512]{2,1,0:T(4,128)S(1)}, f32[8,3,512]{2,1,0:T(4,128)S(1)}, /*index=5*/s32[]{:T(128)}, s32[]{:T(128)}) while((s32[]{:T(128)}, f32[3,256]{1,0:T(4,128)S(1)}, f32[3,256]{1,0:T(4,128)S(1)}, f32[8,3,512]{2,1,0:T(4,128)S(1)}, ...), condition=%wide.region_29.30_spmd.clone, body=%wide.region_25.29_spmd.clone.sunk | while | flops 6161155 | bytes 4261979 | solution.py:57
  285.4 56.3 %reduce-scatter.4.cloned.1.call-done = f32[128,2]{1,0:T(8,128)} async-done(((f32[2048,2]{1,0:T(8,128)}), f32[128,2]{1,0:T(8,128)}) %reduce-scatter.4.cloned.1.call-update) | async-done | bytes 1040
  (324 shorter events, 88.7 us)
Async XLA Ops:
  7.2 117.2 %copy-start.4 = (f32[6,3,256]{2,1,0:T(4,128)S(1)}, f32[6,3,256]{2,1,0:T(4,128)}, u32[]{:S(2)}) copy-start(f32[6,3,256]{2,1,0:T(4,128)} %param.19) | copy-start | bytes 55300
  7.2 334.4 %reduce-scatter.4.cloned.1.call-start = ((), (), s32[]{:S(2)}) async-start(), calls=%async_computation.1 | async-start | bytes 1114112
  7.2 7.2 %collective-permute-start = (f32[6,3,256]{2,1,0:T(4,128)}, f32[6,3,256]{2,1,0:T(4,128)S(1)}, u32[]{:S(2)}, u32[]{:S(2)}) collective-permute-start(f32[6,3,256]{2,1,0:T(4,128)} %param.19), channel_id=1, source_target_pairs={{0,1},{1,2},{2,3},{3,4},{4,5},{5,6},{6,7},{7,8},{8,9},{9,10},{10,1... | collective-permute-start | bytes 55304 | tf_op jit(solution)/shard_map/ppermute | solution.py:16
  14.5 5.9 %collective-permute-start.1 = (f32[6,3,256]{2,1,0:T(4,128)S(1)}, f32[6,3,256]{2,1,0:T(4,128)S(1)}, u32[]{:S(2)}, u32[]{:S(2)}) collective-permute-start(f32[6,3,256]{2,1,0:T(4,128)S(1)} %collective-permute-done), channel_id=1, source_target_pairs={{0,1},{1,2},{2,3},{3,4},{4,5},{5,6},{6,7},{7,8},{8,9},{9,10},{10,1... | collective-permute-start | bytes 55304 | tf_op jit(solution)/shard_map/ppermute | solution.py:16
  20.4 5.9 %collective-permute-start.2 = (f32[6,3,256]{2,1,0:T(4,128)S(1)}, f32[6,3,256]{2,1,0:T(4,128)S(1)}, u32[]{:S(2)}, u32[]{:S(2)}) collective-permute-start(f32[6,3,256]{2,1,0:T(4,128)S(1)} %collective-permute-done.1), channel_id=1, source_target_pairs={{0,1},{1,2},{2,3},{3,4},{4,5},{5,6},{6,7},{7,8},{8,9},{9,10},{10,1... | collective-permute-start | bytes 55304 | tf_op jit(solution)/shard_map/ppermute | solution.py:16
  26.4 5.9 %collective-permute-start.3 = (f32[6,3,256]{2,1,0:T(4,128)S(1)}, f32[6,3,256]{2,1,0:T(4,128)S(1)}, u32[]{:S(2)}, u32[]{:S(2)}) collective-permute-start(f32[6,3,256]{2,1,0:T(4,128)S(1)} %collective-permute-done.2), channel_id=1, source_target_pairs={{0,1},{1,2},{2,3},{3,4},{4,5},{5,6},{6,7},{7,8},{8,9},{9,10},{10,1... | collective-permute-start | bytes 55304 | tf_op jit(solution)/shard_map/ppermute | solution.py:16
  32.3 5.9 %collective-permute-start.4 = (f32[6,3,256]{2,1,0:T(4,128)S(1)}, f32[6,3,256]{2,1,0:T(4,128)S(1)}, u32[]{:S(2)}, u32[]{:S(2)}) collective-permute-start(f32[6,3,256]{2,1,0:T(4,128)S(1)} %collective-permute-done.3), channel_id=1, source_target_pairs={{0,1},{1,2},{2,3},{3,4},{4,5},{5,6},{6,7},{7,8},{8,9},{9,10},{10,1... | collective-permute-start | bytes 55304 | tf_op jit(solution)/shard_map/ppermute | solution.py:16
  38.3 5.9 %collective-permute-start.5 = (f32[6,3,256]{2,1,0:T(4,128)S(1)}, f32[6,3,256]{2,1,0:T(4,128)S(1)}, u32[]{:S(2)}, u32[]{:S(2)}) collective-permute-start(f32[6,3,256]{2,1,0:T(4,128)S(1)} %collective-permute-done.4), channel_id=1, source_target_pairs={{0,1},{1,2},{2,3},{3,4},{4,5},{5,6},{6,7},{7,8},{8,9},{9,10},{10,1... | collective-permute-start | bytes 55304 | tf_op jit(solution)/shard_map/ppermute | solution.py:16
  44.2 5.9 %collective-permute-start.6 = (f32[6,3,256]{2,1,0:T(4,128)S(1)}, f32[6,3,256]{2,1,0:T(4,128)S(1)}, u32[]{:S(2)}, u32[]{:S(2)}) collective-permute-start(f32[6,3,256]{2,1,0:T(4,128)S(1)} %collective-permute-done.5), channel_id=1, source_target_pairs={{0,1},{1,2},{2,3},{3,4},{4,5},{5,6},{6,7},{7,8},{8,9},{9,10},{10,1... | collective-permute-start | bytes 55304 | tf_op jit(solution)/shard_map/ppermute | solution.py:16
  50.2 5.9 %collective-permute-start.7 = (f32[6,3,256]{2,1,0:T(4,128)S(1)}, f32[6,3,256]{2,1,0:T(4,128)S(1)}, u32[]{:S(2)}, u32[]{:S(2)}) collective-permute-start(f32[6,3,256]{2,1,0:T(4,128)S(1)} %collective-permute-done.6), channel_id=1, source_target_pairs={{0,1},{1,2},{2,3},{3,4},{4,5},{5,6},{6,7},{7,8},{8,9},{9,10},{10,1... | collective-permute-start | bytes 55304 | tf_op jit(solution)/shard_map/ppermute | solution.py:16
  56.1 5.9 %collective-permute-start.8 = (f32[6,3,256]{2,1,0:T(4,128)S(1)}, f32[6,3,256]{2,1,0:T(4,128)S(1)}, u32[]{:S(2)}, u32[]{:S(2)}) collective-permute-start(f32[6,3,256]{2,1,0:T(4,128)S(1)} %collective-permute-done.7), channel_id=1, source_target_pairs={{0,1},{1,2},{2,3},{3,4},{4,5},{5,6},{6,7},{7,8},{8,9},{9,10},{10,1... | collective-permute-start | bytes 55304 | tf_op jit(solution)/shard_map/ppermute | solution.py:16
  62.1 5.9 %collective-permute-start.9 = (f32[6,3,256]{2,1,0:T(4,128)S(1)}, f32[6,3,256]{2,1,0:T(4,128)S(1)}, u32[]{:S(2)}, u32[]{:S(2)}) collective-permute-start(f32[6,3,256]{2,1,0:T(4,128)S(1)} %collective-permute-done.8), channel_id=1, source_target_pairs={{0,1},{1,2},{2,3},{3,4},{4,5},{5,6},{6,7},{7,8},{8,9},{9,10},{10,1... | collective-permute-start | bytes 55304 | tf_op jit(solution)/shard_map/ppermute | solution.py:16
  68.0 5.9 %collective-permute-start.10 = (f32[6,3,256]{2,1,0:T(4,128)S(1)}, f32[6,3,256]{2,1,0:T(4,128)S(1)}, u32[]{:S(2)}, u32[]{:S(2)}) collective-permute-start(f32[6,3,256]{2,1,0:T(4,128)S(1)} %collective-permute-done.9), channel_id=1, source_target_pairs={{0,1},{1,2},{2,3},{3,4},{4,5},{5,6},{6,7},{7,8},{8,9},{9,10},{10,1... | collective-permute-start | bytes 55304 | tf_op jit(solution)/shard_map/ppermute | solution.py:16
  74.0 5.9 %collective-permute-start.11 = (f32[6,3,256]{2,1,0:T(4,128)S(1)}, f32[6,3,256]{2,1,0:T(4,128)S(1)}, u32[]{:S(2)}, u32[]{:S(2)}) collective-permute-start(f32[6,3,256]{2,1,0:T(4,128)S(1)} %collective-permute-done.10), channel_id=1, source_target_pairs={{0,1},{1,2},{2,3},{3,4},{4,5},{5,6},{6,7},{7,8},{8,9},{9,10},{10,1... | collective-permute-start | bytes 55304 | tf_op jit(solution)/shard_map/ppermute | solution.py:16
  79.9 5.9 %collective-permute-start.12 = (f32[6,3,256]{2,1,0:T(4,128)S(1)}, f32[6,3,256]{2,1,0:T(4,128)S(1)}, u32[]{:S(2)}, u32[]{:S(2)}) collective-permute-start(f32[6,3,256]{2,1,0:T(4,128)S(1)} %collective-permute-done.11), channel_id=1, source_target_pairs={{0,1},{1,2},{2,3},{3,4},{4,5},{5,6},{6,7},{7,8},{8,9},{9,10},{10,1... | collective-permute-start | bytes 55304 | tf_op jit(solution)/shard_map/ppermute | solution.py:16
  85.9 18.2 %collective-permute-start.13 = (f32[6,3,256]{2,1,0:T(4,128)S(1)}, f32[6,3,256]{2,1,0:T(4,128)S(1)}, u32[]{:S(2)}, u32[]{:S(2)}) collective-permute-start(f32[6,3,256]{2,1,0:T(4,128)S(1)} %collective-permute-done.12), channel_id=1, source_target_pairs={{0,1},{1,2},{2,3},{3,4},{4,5},{5,6},{6,7},{7,8},{8,9},{9,10},{10,1... | collective-permute-start | bytes 55304 | tf_op jit(solution)/shard_map/ppermute | solution.py:16
  104.0 19.0 %collective-permute-start.14 = (f32[6,3,256]{2,1,0:T(4,128)S(1)}, f32[6,3,256]{2,1,0:T(4,128)S(1)}, u32[]{:S(2)}, u32[]{:S(2)}) collective-permute-start(f32[6,3,256]{2,1,0:T(4,128)S(1)} %collective-permute-done.13), channel_id=1, source_target_pairs={{0,1},{1,2},{2,3},{3,4},{4,5},{5,6},{6,7},{7,8},{8,9},{9,10},{10,1... | collective-permute-start | bytes 55304 | tf_op jit(solution)/shard_map/ppermute | solution.py:16
  123.2 1.3 copy-start
  124.5 11.2 %copy-start.5 = (f32[6,3,256]{2,1,0:T(4,128)S(1)}, f32[6,3,256]{2,1,0:T(4,128)}, u32[]{:S(2)}) copy-start(f32[6,3,256]{2,1,0:T(4,128)} %param.20) | copy-start | bytes 55300
  271.6 11.8 %copy-start.1 = (f32[128,3,256]{2,0,1:T(8,128)S(1)}, f32[128,3,256]{2,0,1:T(8,128)}, u32[]{:S(2)}) copy-start(f32[128,3,256]{2,0,1:T(8,128)} %param.21) | copy-start | bytes 1179652
  271.6 11.9 %copy-start.2 = (f32[128,3,256]{2,0,1:T(8,128)S(1)}, f32[128,3,256]{2,0,1:T(8,128)}, u32[]{:S(2)}) copy-start(f32[128,3,256]{2,0,1:T(8,128)} %param.22) | copy-start | bytes 1179652
  282.7 2.6 copy-start.3
Sparse Core Ops, SparseCore 0:
  285.5 56.0 reduce-scatter.3
